TPU v7x, 32 devices: a whole 2x2x4 slice. The times are simulated.
32 devices in a mesh: dp: 8 (over z, y), tensor: 4 (over x, core).
Axes of the slice: x: 2, y: 2, z: 4, core: 2. Of those that a mesh axis runs over, the one named last changes fastest.
Arguments:
- image_rows: bfloat16 [16, 197, 768], P('dp', None, 'tensor'), may hold values from -6 to 6
- text_rows: bfloat16 [8, 512, 768], P('dp', None, 'tensor'), may hold values from -6 to 6
- pair_rows: bfloat16 [8, 711, 768], P('dp', None, 'tensor'), may hold values from -6 to 6
- text_lengths: int32 [8], P('dp'), may hold values from 128 to 512, as said below
- pair_lengths: int32 [8], P('dp'), may hold values from 128 to 512, as said below
- qkv_weight: bfloat16 [3, 768, 3, 768], P(None, None, None, 'tensor'), may hold values from -0.21875 to 0.21875
- qv_bias: bfloat16 [3, 2, 768], P(None, None, 'tensor'), may hold values from -3 to 3
- out_weight: bfloat16 [3, 768, 768], P(None, 'tensor'), may hold values from -3.5 to 3.5
- out_bias: bfloat16 [3, 768], P(None, 'tensor'), may hold values from -3 to 3
- up_weight: bfloat16 [3, 768, 3072], P(None, None, 'tensor'), may hold values from -0.21875 to 0.21875
- up_bias: bfloat16 [3, 3072], P(None, 'tensor'), may hold values from -3 to 3
- down_weight: bfloat16 [3, 3072, 768], P(None, 'tensor'), may hold values from -0.109375 to 0.109375
- down_bias: bfloat16 [3, 768], P(None, 'tensor'), may hold values from -3 to 3
- norm_gain: bfloat16 [3, 2, 768], P(None, None, 'tensor'), may hold values from 0.099609375 to 1.8984375
- norm_bias: bfloat16 [3, 2, 768], P(None, None, 'tensor'), may hold values from -3 to 3
- image_upstream: bfloat16 [16, 197, 768], P('dp', None, 'tensor'), may hold values from -6 to 6
- text_upstream: bfloat16 [8, 512, 768], P('dp', None, 'tensor'), may hold values from -6 to 6
- pair_upstream: bfloat16 [8, 711, 768], P('dp', None, 'tensor'), may hold values from -6 to 6
Outputs:
- image_out: bfloat16 [16, 197, 768], P('dp', None, 'tensor')
- text_out: bfloat16 [8, 512, 768], P('dp', None, 'tensor')
- pair_out: bfloat16 [8, 711, 768], P('dp', None, 'tensor')
- image_input_grad: bfloat16 [16, 197, 768], P('dp', None, 'tensor')
- text_input_grad: bfloat16 [8, 512, 768], P('dp', None, 'tensor')
- pair_input_grad: bfloat16 [8, 711, 768], P('dp', None, 'tensor')
- qkv_grad: float32 [3, 768, 3, 768], P(None, 'dp', None, 'tensor')
- qv_bias_grad: float32 [3, 2, 768], P(None, None, 'tensor')
- out_weight_grad: float32 [3, 768, 768], P(None, 'tensor', 'dp')
- out_bias_grad: float32 [3, 768], P(None, 'tensor')
- up_weight_grad: float32 [3, 768, 3072], P(None, 'dp', 'tensor')
- up_bias_grad: float32 [3, 3072], P(None, 'tensor')
- down_weight_grad: float32 [3, 3072, 768], P(None, 'tensor', 'dp')
- down_bias_grad: float32 [3, 768], P(None, 'tensor')
- norm_gain_grad: float32 [3, 2, 768], P(None, None, 'tensor')
- norm_bias_grad: float32 [3, 2, 768], P(None, None, 'tensor')
Inputs may be any that keep to these rules, and one draw needn't show every extreme that they name: Each text example's first text_lengths rows of 512 are valid; some example of every draw has all 512. Each pair's text rows after its 197 image rows: the first pair_lengths are valid, the rest and the two pad rows are not; some pair of every draw has all 512.
All inputs are finite; a program needn't handle non-finite values.
Results may differ from a plain program's by a relative error of at most 0.017.
Values may be sent and summed in bfloat16 or wider, within the bound.
A program may use at most 192 MiB of HBM per device.

v0:
```python
import math
import jax
import jax.numpy as jnp
from jax import lax
from jax.sharding import PartitionSpec as P

HEAD_DIM = 64
PATCHES = 196
EPSILON = 1e-06


def rounded(value):
    return lax.optimization_barrier(value.astype(jnp.bfloat16)).astype(jnp.float32)


def moments(total_count, square, feature_width):
    mean_val = total_count / feature_width
    return (mean_val, lax.rsqrt(square / feature_width - mean_val * mean_val + EPSILON))


def local_moments(value, feature_width):
    return moments(
        jnp.sum(value, axis=-1, keepdims=True),
        jnp.sum(value * value, axis=-1, keepdims=True),
        feature_width,
    )


def gather_grads(value):
    return lax.all_gather(value, "tensor", axis=2, tiled=True)


def summed_grads(value):
    return lax.psum_scatter(
        rounded(value).astype(jnp.bfloat16), "tensor", scatter_dimension=2, tiled=True
    ).astype(jnp.float32)


def norm_reverse_pass(centered_grad, standardized, inverse_deviation, feature_width):
    total_count, cross_term = lax.psum(
        (
            jnp.sum(centered_grad, axis=-1, keepdims=True),
            jnp.sum(centered_grad * standardized, axis=-1, keepdims=True),
        ),
        "tensor",
    )
    return inverse_deviation * (
        centered_grad - total_count / feature_width - standardized * cross_term / feature_width
    )


def gelu_exact(value):
    return jax.nn.gelu(value, approximate=False)


def masked_scores(queries, key_heads, key_mask, scale):
    scores = (
        jnp.einsum("elhd,emhd->ehlm", queries, key_heads, preferred_element_type=jnp.float32)
        * scale
    )
    return jnp.where(key_mask[:, None, None, :], scores, -1000000000.0)


def forward_tower(row_block, key_mask, weights, tensor_index):
    qkv_w, qv_b, out_w, out_b, up_w, up_b, down_w, down_b, gain, shift = weights
    feature_width = qkv_w.shape[0]
    share = out_w.shape[0]
    examples = row_block.shape[0]
    length = row_block.shape[1]
    head_count = share // HEAD_DIM
    scale = 1.0 / math.sqrt(HEAD_DIM)
    rows_float = row_block.astype(jnp.float32)
    whole_rows, whole_bias, whole_gain, whole_shift = (
        lax.all_gather(row_block, "tensor", axis=2, tiled=True),
        lax.all_gather(out_b, "tensor", axis=0, tiled=True),
        lax.all_gather(gain, "tensor", axis=1, tiled=True),
        lax.all_gather(shift, "tensor", axis=1, tiled=True),
    )
    whole_f = whole_rows.astype(jnp.float32)
    input_mean, input_inverse_deviation = local_moments(whole_f, feature_width)
    normed = (
        (whole_f - input_mean) * input_inverse_deviation * whole_gain[0].astype(jnp.float32)
        + whole_shift[0].astype(jnp.float32)
    ).astype(jnp.bfloat16)
    projected = jnp.einsum("eld,dcf->elcf", normed, qkv_w, preferred_element_type=jnp.float32)
    queries = (
        (projected[:, :, 0] + qv_b[0].astype(jnp.float32))
        .astype(jnp.bfloat16)
        .reshape(examples, length, head_count, HEAD_DIM)
    )
    key_heads = (
        projected[:, :, 1].astype(jnp.bfloat16).reshape(examples, length, head_count, HEAD_DIM)
    )
    value_heads = (
        (projected[:, :, 2] + qv_b[1].astype(jnp.float32))
        .astype(jnp.bfloat16)
        .reshape(examples, length, head_count, HEAD_DIM)
    )
    scores = masked_scores(queries, key_heads, key_mask, scale)
    top_score = jnp.max(scores, axis=-1, keepdims=True)
    log_total = top_score + jnp.log(jnp.sum(jnp.exp(scores - top_score), axis=-1, keepdims=True))
    probs_low = jnp.exp(scores - log_total).astype(jnp.bfloat16)
    mixed = (
        jnp.einsum("ehlm,emhd->elhd", probs_low, value_heads, preferred_element_type=jnp.float32)
        .astype(jnp.bfloat16)
        .reshape(examples, length, share)
    )
    partial_value = jnp.einsum("elf,fd->eld", mixed, out_w, preferred_element_type=jnp.float32)
    attn_full = lax.psum(rounded(partial_value).astype(jnp.bfloat16), "tensor").astype(
        jnp.float32
    ) + whole_bias.astype(jnp.float32)
    resid_full = whole_f + attn_full
    middle_mean, middle_inverse_deviation = local_moments(resid_full, feature_width)
    normed_two = (
        (resid_full - middle_mean) * middle_inverse_deviation * whole_gain[1].astype(jnp.float32)
        + whole_shift[1].astype(jnp.float32)
    ).astype(jnp.bfloat16)
    attention = lax.dynamic_slice_in_dim(attn_full, tensor_index * share, share, 2)
    residual_stream = rows_float + attention
    hidden = jnp.einsum(
        "eld,df->elf", normed_two, up_w, preferred_element_type=jnp.float32
    ) + up_b.astype(jnp.float32)
    activated = gelu_exact(hidden).astype(jnp.bfloat16)
    down_part = jnp.einsum("elf,fd->eld", activated, down_w, preferred_element_type=jnp.float32)
    feedforward = lax.psum_scatter(
        rounded(down_part).astype(jnp.bfloat16), "tensor", scatter_dimension=2, tiled=True
    ).astype(jnp.float32) + down_b.astype(jnp.float32)
    output = residual_stream + feedforward
    kept = (
        normed,
        queries,
        key_heads,
        value_heads,
        log_total,
        mixed,
        normed_two,
        hidden,
        activated,
        input_mean,
        input_inverse_deviation,
        middle_mean,
        middle_inverse_deviation,
        residual_stream,
        rows_float,
    )
    return (output, kept)


def backward_tower(upstream, weights, kept, key_mask):
    qkv_w, qv_b, out_w, out_b, up_w, up_b, down_w, down_b, gain, shift = weights
    (
        normed,
        queries,
        key_heads,
        value_heads,
        log_total,
        mixed,
        normed_two,
        hidden,
        activated,
        input_mean,
        input_inverse_deviation,
        middle_mean,
        middle_inverse_deviation,
        residual_stream,
        rows_float,
    ) = kept
    feature_width = qkv_w.shape[0]
    share = out_w.shape[0]
    examples = queries.shape[0]
    length = queries.shape[1]
    head_count = share // HEAD_DIM
    scale = 1.0 / math.sqrt(HEAD_DIM)
    gain_float = gain.astype(jnp.float32)
    output_gradient = upstream.astype(jnp.float32)
    grad_ffn = output_gradient.astype(jnp.bfloat16)
    down_bias_grad = jnp.sum(grad_ffn, axis=(0, 1), dtype=jnp.float32)
    ffn_full = gather_grads(grad_ffn)
    down_grad = jnp.einsum("elf,eld->fd", activated, ffn_full, preferred_element_type=jnp.float32)
    grad_act = jnp.einsum("eld,fd->elf", ffn_full, down_w, preferred_element_type=jnp.float32)
    grad_hidden = jax.vjp(gelu_exact, hidden)[1](grad_act)[0].astype(jnp.bfloat16)
    up_bias_grad = jnp.sum(grad_hidden, axis=(0, 1), dtype=jnp.float32)
    up_grad = jnp.einsum("eld,elf->df", normed_two, grad_hidden, preferred_element_type=jnp.float32)
    second_normed_gradient = summed_grads(
        jnp.einsum("elf,df->eld", grad_hidden, up_w, preferred_element_type=jnp.float32)
    )
    standardized_middle = (residual_stream - middle_mean) * middle_inverse_deviation
    middle_gain_grad = jnp.sum(second_normed_gradient * standardized_middle, axis=(0, 1))
    shift_mid_grad = jnp.sum(second_normed_gradient, axis=(0, 1))
    residual_gradient = output_gradient + norm_reverse_pass(
        second_normed_gradient * gain_float[1],
        standardized_middle,
        middle_inverse_deviation,
        feature_width,
    )
    grad_attn = residual_gradient.astype(jnp.bfloat16)
    out_bias_grad = jnp.sum(grad_attn, axis=(0, 1), dtype=jnp.float32)
    attn_full = gather_grads(grad_attn)
    out_grad = jnp.einsum("elf,eld->fd", mixed, attn_full, preferred_element_type=jnp.float32)
    grad_mixed = (
        jnp.einsum("eld,fd->elf", attn_full, out_w, preferred_element_type=jnp.float32)
        .astype(jnp.bfloat16)
        .reshape(examples, length, head_count, HEAD_DIM)
    )
    scores = masked_scores(queries, key_heads, key_mask, scale)
    probs_f = jnp.exp(scores - log_total)
    probs_low = probs_f.astype(jnp.bfloat16)
    grad_values = jnp.einsum(
        "ehlm,elhd->emhd", probs_low, grad_mixed, preferred_element_type=jnp.float32
    ).astype(jnp.bfloat16)
    grad_probs = jnp.einsum(
        "elhd,emhd->ehlm", grad_mixed, value_heads, preferred_element_type=jnp.float32
    )
    grad_scores = (
        probs_f * (grad_probs - jnp.sum(probs_f * grad_probs, axis=-1, keepdims=True))
    ).astype(jnp.bfloat16)
    grad_queries = (
        jnp.einsum("ehlm,emhd->elhd", grad_scores, key_heads, preferred_element_type=jnp.float32)
        * scale
    ).astype(jnp.bfloat16)
    grad_keys = (
        jnp.einsum("ehlm,elhd->emhd", grad_scores, queries, preferred_element_type=jnp.float32)
        * scale
    ).astype(jnp.bfloat16)
    grad_qkv = jnp.stack([grad_queries, grad_keys, grad_values], 2).reshape(
        examples, length, 3, share
    )
    qv_bias_grad = jnp.stack(
        [
            jnp.sum(grad_qkv[:, :, 0], axis=(0, 1), dtype=jnp.float32),
            jnp.sum(grad_qkv[:, :, 2], axis=(0, 1), dtype=jnp.float32),
        ],
        0,
    )
    qkv_grad = jnp.einsum("eld,elcf->dcf", normed, grad_qkv, preferred_element_type=jnp.float32)
    normed_gradient = summed_grads(
        jnp.einsum("elcf,dcf->eld", grad_qkv, qkv_w, preferred_element_type=jnp.float32)
    )
    standardized_input = (rows_float - input_mean) * input_inverse_deviation
    input_gain_grad = jnp.sum(normed_gradient * standardized_input, axis=(0, 1))
    shift_in_grad = jnp.sum(normed_gradient, axis=(0, 1))
    grad_input = (
        residual_gradient
        + norm_reverse_pass(
            normed_gradient * gain_float[0],
            standardized_input,
            input_inverse_deviation,
            feature_width,
        )
    ).astype(jnp.bfloat16)
    small_grads = jnp.concatenate(
        [
            qv_bias_grad,
            out_bias_grad[None],
            up_bias_grad.reshape(-1, share),
            down_bias_grad[None],
            jnp.stack([input_gain_grad, middle_gain_grad], 0),
            jnp.stack([shift_in_grad, shift_mid_grad], 0),
        ],
        0,
    )
    return (grad_input, (qkv_grad, out_grad, up_grad, down_grad, small_grads))


def per_device(
    image_rows,
    text_rows,
    pair_rows,
    text_lengths,
    pair_lengths,
    qkv_weight,
    qv_bias,
    out_weight,
    out_bias,
    up_weight,
    up_bias,
    down_weight,
    down_bias,
    norm_gain,
    norm_bias,
    image_upstream,
    text_upstream,
    pair_upstream,
):
    tensor_index = lax.axis_index("tensor")
    image_mask = jnp.ones((image_rows.shape[0], image_rows.shape[1]), dtype=bool)
    text_mask = jnp.arange(text_rows.shape[1], dtype=jnp.int32)[None, :] < text_lengths[:, None]
    pair_mask = jnp.arange(pair_rows.shape[1], dtype=jnp.int32)[None, :] < pair_lengths[:, None] + (
        PATCHES + 1
    )
    towers_in = (
        (image_rows, image_mask, image_upstream),
        (text_rows, text_mask, text_upstream),
        (pair_rows, pair_mask, pair_upstream),
    )
    params = (
        qkv_weight,
        qv_bias,
        out_weight,
        out_bias,
        up_weight,
        up_bias,
        down_weight,
        down_bias,
        norm_gain,
        norm_bias,
    )
    outputs = []
    input_grads = []
    grad_lists = ([], [], [], [], [])
    for tower_id in range(3):
        row_block, key_mask, upstream = towers_in[tower_id]
        weights = tuple((entry[tower_id] for entry in params))
        output, kept = forward_tower(row_block, key_mask, weights, tensor_index)
        outputs.append(output.astype(jnp.bfloat16))
        grad_input, grads = backward_tower(upstream, weights, kept, key_mask)
        input_grads.append(grad_input)
        for slot_id in range(5):
            grad_lists[slot_id].append(grads[slot_id])
    stacked = tuple((jnp.stack(group_list, 0) for group_list in grad_lists))
    qkv_grad, out_weight_grad, up_weight_grad, down_weight_grad = (
        lax.psum_scatter(stacked[0], "dp", scatter_dimension=1, tiled=True),
        lax.psum_scatter(stacked[1], "dp", scatter_dimension=2, tiled=True),
        lax.psum_scatter(stacked[2], "dp", scatter_dimension=1, tiled=True),
        lax.psum_scatter(stacked[3], "dp", scatter_dimension=2, tiled=True),
    )
    small_grads = lax.psum(stacked[4], "dp")
    share = out_weight.shape[1]
    hidden_share = up_weight.shape[2]
    ratio = hidden_share // share
    qv_bias_grad = small_grads[:, 0:2]
    out_bias_grad = small_grads[:, 2]
    up_bias_grad = small_grads[:, 3 : 3 + ratio].reshape(3, hidden_share)
    down_bias_grad = small_grads[:, 3 + ratio]
    norm_gain_grad = small_grads[:, 4 + ratio : 6 + ratio]
    norm_bias_grad = small_grads[:, 6 + ratio : 8 + ratio]
    return (
        outputs[0],
        outputs[1],
        outputs[2],
        input_grads[0],
        input_grads[1],
        input_grads[2],
        qkv_grad,
        qv_bias_grad,
        out_weight_grad,
        out_bias_grad,
        up_weight_grad,
        up_bias_grad,
        down_weight_grad,
        down_bias_grad,
        norm_gain_grad,
        norm_bias_grad,
    )


def solution(mesh):
    return jax.shard_map(
        per_device,
        mesh=mesh,
        in_specs=(
            P("dp", None, "tensor"),
            P("dp", None, "tensor"),
            P("dp", None, "tensor"),
            P("dp"),
            P("dp"),
            P(None, None, None, "tensor"),
            P(None, None, "tensor"),
            P(None, "tensor", None),
            P(None, "tensor"),
            P(None, None, "tensor"),
            P(None, "tensor"),
            P(None, "tensor", None),
            P(None, "tensor"),
            P(None, None, "tensor"),
            P(None, None, "tensor"),
            P("dp", None, "tensor"),
            P("dp", None, "tensor"),
            P("dp", None, "tensor"),
        ),
        out_specs=(
            P("dp", None, "tensor"),
            P("dp", None, "tensor"),
            P("dp", None, "tensor"),
            P("dp", None, "tensor"),
            P("dp", None, "tensor"),
            P("dp", None, "tensor"),
            P(None, "dp", None, "tensor"),
            P(None, None, "tensor"),
            P(None, "tensor", "dp"),
            P(None, "tensor"),
            P(None, "dp", "tensor"),
            P(None, "tensor"),
            P(None, "tensor", "dp"),
            P(None, "tensor"),
            P(None, None, "tensor"),
            P(None, None, "tensor"),
        ),
        check_vma=False,
    )
```

profile of v0, /device:TPU:0, one launch (start us, length us, event | category | flops | bytes accessed | tf_op | source)
XLA Modules:
  0.0 1013.4 jit_solution(11684703509112066378)
XLA Ops:
  8.7 7.9 all-gather.1
  16.7 5.3 fusion.178
  23.4 6.6 all-gather
  30.0 5.3 fusion.179
  35.5 8.7 all_gather.54
  56.0 12.3 %all_gather.58 = bf16[1,512,768]{1,2,0:T(8,128)(2,1)S(1)} all-gather(bf16[1,512,192]{1,2,0:T(8,128)(2,1)S(1)} %copy-done.81), channel_id=1, replica_groups=mesh['dp'=8,'tensor'=4] {'tensor'}, dimensions={2}, use_global_device_ids=true | all-gather | bytes 983040 | tf_op jit(solution)/shard_map/all_gather | solution.py:74
  68.7 6.6 all-gather.4
  75.3 5.3 fusion.174
  80.8 8.5 all-gather.3
  89.3 5.3 fusion.175
  100.1 8.3 all-reduce.8
  122.7 6.1 all-gather.7
  128.8 4.7 fusion.170
  133.7 6.6 all-gather.6
  140.3 4.7 fusion.171
  145.3 9.7 all_gather.66
  160.3 3.6 multiply_convert_fusion.5
  192.1 10.5 %all_gather.68 = bf16[1,512,768]{1,2,0:T(8,128)(2,1)} all-gather(bf16[1,512,192]{1,2,0:T(8,128)(2,1)S(1)} %copy-done.82), channel_id=1, replica_groups=mesh['dp'=8,'tensor'=4] {'tensor'}, dimensions={2}, use_global_device_ids=true | all-gather | bytes 983040 | tf_op jit(solution)/shard_map/all_gather | solution.py:30
  202.6 51.6 %all-reduce.19.cloned.1.call-done = (bf16[1,512,768]{2,1,0:T(8,128)(2,1)}, bf16[1,711,768]{2,1,0:T(8,128)(2,1)}, bf16[2,197,768]{1,0,2:T(2,128)(2,1)}) async-done(((bf16[1,512,768]{2,1,0:T(8,128)(2,1)}, bf16[1,711,768]{2,1,0:T(8,128)(2,1)}, bf16[2,197,768]{1,0,2:T(2,128)(2,1)}), (bf16[1,512,768]{2,1,0:T(8,128)(2,1)}, bf16[1,711,768]{2,1,0:T(8,128)(2,1)}, ...) | async-done | bytes 2483728 | tf_op jit(solution)/shard_map/psum | solution.py:109
  257.3 6.4 multiply_convert_fusion.3
  270.6 4.7 copy.225
  281.1 4.8 copy.221
  290.5 9.1 multiply_convert_fusion.2
  299.6 5.4 convert_reduce_fusion.2
  306.0 3.3 fusion.28
  309.3 6.7 copy.229
  332.4 4.5 slice_reduce_fusion.4
  336.9 4.5 slice_reduce_fusion.2
  341.4 4.5 slice_reduce_fusion
  356.0 3.6 fusion.27
  359.6 6.7 copy.223
  389.0 11.6 %all-reduce.7 = (f32[2,197]{1,0:T(2,128)}, f32[2,197,1]{1,0,2:T(2,128)}, f32[512]{0:T(512)}, f32[1,512,1]{1,2,0:T(1,128)}, f32[711]{0:T(1024)}, /*index=5*/f32[1,711,1]{1,2,0:T(1,128)}) all-reduce(f32[2,197]{1,0:T(2,128)} %get-tuple-element.87, f32[2,197,1]{1,0,2:T(2,128)} %bitcast.503, ...), channel_id=1, replica_groups=mesh['dp'=8,'tensor'=4] {'tensor'}, use_global_device_ids=true, to_apply=%region_28.29 | all-reduce | flops 3234 | bytes 25872 | tf_op jit(solution)/shard_map/psum | solution.py:40
  406.0 9.1 all_gather.67
  427.3 3.6 convert_reduce_fusion.17
  437.5 4.1 convert_reduce_fusion.11
  443.5 9.0 all_gather.69
  473.2 5.3 multiply_reduce_fusion
  504.3 3.3 pad_maximum_fusion.1
  507.6 11.0 %copy.237 = f32[3,768,768]{1,0,2:T(4,128)} copy(f32[3,768,768]{2,1,0:T(8,128)} %pad_maximum_fusion.1) | data formatting | bytes 14155776
  518.5 8.2 copy.255
  535.6 9.8 copy.233
  545.4 11.3 %reshape.1241 = f32[768,1728]{1,0:T(8,128)} reshape(f32[768,3,3,192]{3,2,1,0:T(4,128)} %bitcast.422) | data formatting | bytes 10616832
  563.0 3.4 pad_maximum_fusion
  577.5 10.9 %all-reduce.6 = (f32[2,197]{1,0:T(2,128)S(1)}, f32[2,197,1]{1,0,2:T(2,128)S(1)}, f32[512]{0:T(512)S(1)}, f32[1,512,1]{1,2,0:T(1,128)S(1)}, f32[711]{0:T(1024)S(1)}, /*index=5*/f32[1,711,1]{1,2,0:T(1,128)S(1)}) all-reduce(f32[2,197]{1,0:T(2,128)S(1)} %get-tuple-element.105, ...), channel_id=1, replica_groups=mesh['dp'=8,'tensor'=4] {'tensor'}, use_global_device_ids=true, to_apply=%region_34.35 | all-reduce | flops 3234 | bytes 25872 | tf_op jit(solution)/shard_map/psum | solution.py:40
  597.3 38.3 %psum.127 = f32[3,12,192]{2,1,0:T(8,128)S(1)} all-reduce(f32[3,12,192]{2,1,0:T(8,128)S(1)} %pad_maximum_fusion.9), channel_id=1, replica_groups=mesh['dp'=8,'tensor'=4] {'dp'}, use_global_device_ids=true, to_apply=%region_85.86 | all-reduce | flops 6912 | bytes 55296 | tf_op jit(solution)/shard_map/psum | solution.py:327
  639.6 124.9 %reduce-scatter.47.cloned.1.call-done = f32[96,2304]{1,0:T(8,128)} async-done(((f32[768,2304]{1,0:T(8,128)}), f32[96,2304]{1,0:T(8,128)}) %reduce-scatter.47.cloned.1.call-update) | async-done | bytes 884752
  767.2 106.9 %reduce-scatter.43.cloned.1.call-done = f32[96,1728]{1,0:T(8,128)} async-done(((f32[768,1728]{1,0:T(8,128)}), f32[96,1728]{1,0:T(8,128)}) %reduce-scatter.43.cloned.1.call-update) | async-done | bytes 663568
  876.9 129.8 %reduce-scatter.29.cloned.1.call-done = f32[3,96,768]{2,1,0:T(8,128)} async-done(((f32[3,768,768]{2,1,0:T(8,128)}), f32[3,96,768]{2,1,0:T(8,128)}) %reduce-scatter.29.cloned.1.call-update) | async-done | bytes 884752 | tf_op jit(solution)/shard_map/reduce_scatter | solution.py:324
  (700 shorter events, 251.6 us)
Async XLA Ops:
  7.2 28.1 %copy-start.77 = (bf16[2,197,192]{1,2,0:T(8,128)(2,1)S(1)}, bf16[2,197,192]{1,2,0:T(8,128)(2,1)}, u32[]{:S(2)}) copy-start(bf16[2,197,192]{1,2,0:T(8,128)(2,1)} %param.18) | copy-start | bytes 453892
  7.2 147.8 %all-reduce.15.cloned.1.call-start = ((), (), s32[]{:S(2)}) async-start(), calls=%async_computation.10 | async-start | bytes 1228800 | tf_op jit(solution)/shard_map/psum | solution.py:109
  22.0 23.2 %copy-start.166 = (f32[768]{0:T(1024)}, f32[768]{0:T(1024)S(1)}, u32[]{:S(2)}) copy-start(f32[768]{0:T(1024)S(1)} %get-tuple-element.116) | copy-start | bytes 9220
  52.7 120.8 %all-gather.13.cloned.1.call-start = ((), (), s32[]{:S(2)}) async-start(), calls=%async_computation.11 | async-start | bytes 1474560 | tf_op jit(solution)/shard_map/all_gather | solution.py:74
  53.4 200.8 %all-reduce.19.cloned.1.call-start = ((), (), s32[]{:S(2)}) async-start(), calls=%async_computation.25 | async-start | bytes 5332992 | tf_op jit(solution)/shard_map/psum | solution.py:109
  68.6 26.4 %copy-start.11 = (bf16[1,512,768]{2,1,0:T(8,128)(2,1)}, bf16[1,512,768]{2,1,0:T(8,128)(2,1)S(1)}, u32[]{:S(2)}) copy-start(bf16[1,512,768]{2,1,0:T(8,128)(2,1)S(1)} %copy.164) | copy-start | bytes 2359300
  80.6 15.3 %copy-start.174 = (f32[768]{0:T(1024)}, f32[768]{0:T(1024)S(1)}, u32[]{:S(2)}) copy-start(f32[768]{0:T(1024)S(1)} %get-tuple-element.112) | copy-start | bytes 9220
  80.8 15.1 %copy-start.68 = (bf16[1,2,192]{1,0,2:T(2,128)(2,1)}, bf16[1,2,192]{1,0,2:T(2,128)(2,1)S(1)}, u32[]{:S(2)}) copy-start(bf16[1,2,192]{1,0,2:T(2,128)(2,1)S(1)} %copy.251) | copy-start | bytes 2308
  97.4 14.2 %copy-start.25 = (f32[1,512,1,192]{1,3,2,0:T(8,128)}, f32[1,512,1,192]{1,3,2,0:T(8,128)S(1)}, u32[]{:S(2)}) copy-start(f32[1,512,1,192]{1,3,2,0:T(8,128)S(1)} %get-tuple-element.191) | copy-start | bytes 1179652
  118.2 15.4 %copy-start.199 = (bf16[1,2,192]{2,1,0:T(2,128)(2,1)S(1)}, bf16[1,2,192]{2,1,0:T(2,128)(2,1)}, u32[]{:S(2)}) copy-start(bf16[1,2,192]{2,1,0:T(2,128)(2,1)} %get-tuple-element.209) | copy-start | bytes 2308
  121.1 24.0 %copy-start.203 = (f32[192]{0:T(256)S(1)}, f32[192]{0:T(256)}, u32[]{:S(2)}) copy-start(f32[192]{0:T(256)} %get-tuple-element.144) | copy-start | bytes 2308
  121.1 24.1 %copy-start.202 = (f32[192]{0:T(256)S(1)}, f32[192]{0:T(256)}, u32[]{:S(2)}) copy-start(f32[192]{0:T(256)} %get-tuple-element.139) | copy-start | bytes 2308
  121.1 24.1 %copy-start.83 = (bf16[2,197,192]{1,2,0:T(8,128)(2,1)S(1)}, bf16[2,197,192]{1,2,0:T(8,128)(2,1)}, u32[]{:S(2)}) copy-start(bf16[2,197,192]{1,2,0:T(8,128)(2,1)} %param.33) | copy-start | bytes 453892
  121.8 61.7 %copy-start.110 = (pred[711]{0:T(1024)(128)(4,1)}, pred[711]{0:T(1024)(128)(4,1)S(1)}, u32[]{:S(2)}) copy-start(pred[711]{0:T(1024)(128)(4,1)S(1)} %iota_compare_fusion) | copy-start | bytes 2137
  128.8 26.2 %copy-start.140 = (f32[768]{0:T(1024)S(1)}, f32[768]{0:T(1024)}, u32[]{:S(2)}) copy-start(f32[768]{0:T(1024)} %convert_element_type.887) | copy-start | bytes 9220
  133.5 44.0 %copy-start.182 = (f32[768]{0:T(1024)}, f32[768]{0:T(1024)S(1)}, u32[]{:S(2)}) copy-start(f32[768]{0:T(1024)S(1)} %get-tuple-element.108) | copy-start | bytes 9220
  133.5 156.9 %copy-start.178 = (f32[768]{0:T(1024)}, f32[768]{0:T(1024)S(1)}, u32[]{:S(2)}) copy-start(f32[768]{0:T(1024)S(1)} %get-tuple-element.109) | copy-start | bytes 9220
  133.7 24.0 %copy-start.70 = (bf16[1,2,192]{1,0,2:T(2,128)(2,1)}, bf16[1,2,192]{1,0,2:T(2,128)(2,1)S(1)}, u32[]{:S(2)}) copy-start(bf16[1,2,192]{1,0,2:T(2,128)(2,1)S(1)} %copy.253) | copy-start | bytes 2308
  145.0 32.5 %copy-start.184 = (f32[768]{0:T(1024)}, f32[768]{0:T(1024)S(1)}, u32[]{:S(2)}) copy-start(f32[768]{0:T(1024)S(1)} %get-tuple-element.106) | copy-start | bytes 9220
  145.1 145.4 %copy-start.180 = (f32[768]{0:T(1024)}, f32[768]{0:T(1024)S(1)}, u32[]{:S(2)}) copy-start(f32[768]{0:T(1024)S(1)} %get-tuple-element.107) | copy-start | bytes 9220
  145.2 35.2 %copy-start.134 = (f32[3,64]{1,0:T(4,128)}, f32[3,64]{1,0:T(4,128)S(1)}, u32[]{:S(2)}) copy-start(f32[3,64]{1,0:T(4,128)S(1)} %reshape.1120) | copy-start | bytes 2308
  145.2 41.0 %copy-start.136 = (f32[3,64]{1,0:T(4,128)}, f32[3,64]{1,0:T(4,128)S(1)}, u32[]{:S(2)}) copy-start(f32[3,64]{1,0:T(4,128)S(1)} %reshape.1119) | copy-start | bytes 2308
  191.2 108.4 %all-gather.15.cloned.1.call-start = ((), (), s32[]{:S(2)}) async-start(), calls=%async_computation.12 | async-start | bytes 1474560 | tf_op jit(solution)/shard_map/all_gather | solution.py:30
  191.8 179.9 %reduce-scatter.35.cloned.1.call-start = ((), (), s32[]{:S(2)}) async-start(), calls=%async_computation.17 | async-start | bytes 983040
  192.1 65.1 %copy-start.142 = (f32[768]{0:T(1024)}, f32[768]{0:T(1024)S(1)}, u32[]{:S(2)}) copy-start(f32[768]{0:T(1024)S(1)} %convert_element_type.888) | copy-start | bytes 9220
  277.9 97.5 %reduce-scatter.31.cloned.1.call-start = ((), (), s32[]{:S(2)}) async-start(), calls=%async_computation.15 | async-start | bytes 983040
  277.9 12.6 %copy-start.144 = (f32[768]{0:T(1024)}, f32[768]{0:T(1024)S(1)}, u32[]{:S(2)}) copy-start(f32[768]{0:T(1024)S(1)} %convert_element_type.889) | copy-start | bytes 9220
  290.4 91.2 %reduce-scatter.39.cloned.1.call-start = ((), (), s32[]{:S(2)}) async-start(), calls=%async_computation.19 | async-start | bytes 1474560
  318.9 114.5 %reduce-scatter.33.cloned.1.call-start = ((), (), s32[]{:S(2)}) async-start(), calls=%async_computation.16 | async-start | bytes 1474560
  322.7 23.3 %copy-start.161 = (bf16[3,192]{1,0:T(4,128)(2,1)S(1)}, bf16[3,192]{1,0:T(4,128)(2,1)}, u32[]{:S(2)}) copy-start(bf16[3,192]{1,0:T(4,128)(2,1)} %param.30) | copy-start | bytes 3460
  324.6 112.9 %copy-start.9 = (bf16[1,711,192]{2,1,0:T(8,128)(2,1)}, bf16[1,711,192]{2,1,0:T(8,128)(2,1)S(1)}, u32[]{:S(2)}) copy-start(bf16[1,711,192]{2,1,0:T(8,128)(2,1)S(1)} %copy.168) | copy-start | bytes 819076
  336.9 32.3 %copy-start.138 = (f32[192]{0:T(256)}, f32[192]{0:T(256)S(1)}, u32[]{:S(2)}) copy-start(f32[192]{0:T(256)S(1)} %get-tuple-element.135) | copy-start | bytes 2308
  369.2 100.9 %all-gather.17.cloned.1.call-start = ((), (), s32[]{:S(2)}) async-start(), calls=%async_computation.13 | async-start | bytes 1474560 | tf_op jit(solution)/shard_map/all_gather | solution.py:30
  401.2 15.3 %copy-start.121 = (f32[2,197]{1,0:T(2,128)}, f32[2,197]{1,0:T(2,128)S(1)}, u32[]{:S(2)}) copy-start(f32[2,197]{1,0:T(2,128)S(1)} %multiply_bitcast_fusion.1) | copy-start | bytes 4732
  443.5 125.9 %all-reduce.17.cloned.1.call-start = ((), (), s32[]{:S(2)}) async-start(), calls=%async_computation.24 | async-start | bytes 3145728
  459.6 112.8 %reduce-scatter.37.cloned.1.call-start = ((), (), s32[]{:S(2)}) async-start(), calls=%async_computation.18 | async-start | bytes 983040
  469.9 104.9 %reduce-scatter.41.cloned.1.call-start = ((), (), s32[]{:S(2)}) async-start(), calls=%async_computation.20 | async-start | bytes 1474560
  489.9 147.6 %reduce-scatter.45.cloned.1.call-start = ((), (), s32[]{:S(2)}) async-start(), calls=%async_computation.22 | async-start | bytes 2211840
  499.4 265.1 %reduce-scatter.47.cloned.1.call-start = ((), (), s32[]{:S(2)}) async-start(), calls=%async_computation.23 | async-start | bytes 7962624
  526.8 347.3 %reduce-scatter.43.cloned.1.call-start = ((), (), s32[]{:S(2)}) async-start(), calls=%async_computation.21 | async-start | bytes 6193152
  556.8 449.9 %reduce-scatter.29.cloned.1.call-start = ((), (), s32[]{:S(2)}) async-start(), calls=%async_computation.14 | async-start | bytes 7962624 | tf_op jit(solution)/shard_map/reduce_scatter | solution.py:324
  574.0 14.4 %copy-start.35 = (bf16[2,197,192]{2,1,0:T(8,128)(2,1)S(1)}, bf16[2,197,192]{2,1,0:T(8,128)(2,1)}, u32[]{:S(2)}) copy-start(bf16[2,197,192]{2,1,0:T(8,128)(2,1)} %copy.175) | copy-start | bytes 453892
  574.0 14.4 %copy-start.47 = (bf16[2,197,192]{2,1,0:T(8,128)(2,1)S(1)}, bf16[2,197,192]{2,1,0:T(8,128)(2,1)}, u32[]{:S(2)}) copy-start(bf16[2,197,192]{2,1,0:T(8,128)(2,1)} %copy.173) | copy-start | bytes 453892
  574.0 14.4 %copy-start.122 = (f32[2,197]{1,0:T(2,128)S(1)}, f32[2,197]{1,0:T(2,128)}, u32[]{:S(2)}) copy-start(f32[2,197]{1,0:T(2,128)} %copy-done.121) | copy-start | bytes 4732
  574.0 14.4 %copy-start.139 = (f32[192]{0:T(256)S(1)}, f32[192]{0:T(256)}, u32[]{:S(2)}) copy-start(f32[192]{0:T(256)} %copy-done.138) | copy-start | bytes 2308
  574.1 14.4 %copy-start.159 = (f32[2,197]{1,0:T(2,128)S(1)}, f32[2,197]{1,0:T(2,128)}, u32[]{:S(2)}) copy-start(f32[2,197]{1,0:T(2,128)} %get-tuple-element.154) | copy-start | bytes 4732
  574.1 14.4 %copy-start.198 = (f32[1,192]{1,0:T(1,128)S(1)}, f32[1,192]{1,0:T(1,128)}, u32[]{:S(2)}) copy-start(f32[1,192]{1,0:T(1,128)} %get-tuple-element.216) | copy-start | bytes 2308
  576.9 17.7 %copy-start.46 = (f32[1,512,192]{2,1,0:T(8,128)S(1)}, f32[1,512,192]{2,1,0:T(8,128)}, u32[]{:S(2)}) copy-start(f32[1,512,192]{2,1,0:T(8,128)} %get-tuple-element.172) | copy-start | bytes 1179652
  (192 other events, 570.3 us)
Sparse Core Ops, SparseCore 0:
  52.8 36.7 all-reduce.14
  91.1 18.1 all-gather.12
  191.3 62.8 all-reduce.18
  255.6 17.4 all-gather.14
  278.0 23.3 reduce-scatter.34
  303.8 23.2 reduce-scatter.30
  329.6 25.6 reduce-scatter.38
  369.3 25.7 reduce-scatter.32
  443.6 17.4 all-gather.16
  464.5 42.8 all-reduce.16
  509.9 23.2 reduce-scatter.36
  535.6 25.6 reduce-scatter.40
  564.8 67.8 reduce-scatter.44
  636.2 128.2 reduce-scatter.46
  768.0 106.0 reduce-scatter.42
  878.2 128.5 reduce-scatter.28
where the time goes:
time: 1030 us; the launch traced here: 1010 us
  waiting for transfers between devices  415 us (40%)
  local copies, waits for them, and re-layouts  204 us (20%)
  blocking collectives  171 us (17%)
  matrix products  106 us (10%)
  other arithmetic  96.2 us (9%)
  between operations  19.5 us (2%)
    unnamed x26, waiting for transfers between devices  233 us
    unnamed x514, local copies, waits for them, and re-layouts  160 us
    reduce_scatter x1, waiting for transfers between devices, per_device(): lax.psum_scatter(stacked[2], 'dp', scatter_dimension=1, tiled=True)  130 us
    psum x2, waiting for transfers between devices, forward_tower(): lax.psum(rounded(partial_value).astype(jnp.bfloat16), 'tensor')  51.6 us
    all_gather x4, blocking collectives, gather_grads(): return lax.all_gather(value, 'tensor', axis=2, tiled=True)  38.4 us
    psum x1, blocking collectives, per_device(): small_grads = lax.psum(stacked[4], 'dp')  38.3 us
    psum x2, blocking collectives, norm_reverse_pass(): lax.psum((jnp.sum(centered_grad, axis=-1, keepdims=True), jnp.sum(centere...  22.5 us
    all_gather x3, blocking collectives, forward_tower(): lax.all_gather(gain, 'tensor', axis=1, tiled=True)  21.7 us
  transfers between devices with their start and end apart: 16, of which 4 were waited for; matrix products, arithmetic and copies ran while one was open for 34% of the time, Pallas kernels for 0%

commit v1 on v0

--- a/solution.py
+++ b/solution.py
@@ -1,12 +1,45 @@
+import functools
 import math
 import jax
 import jax.numpy as jnp
 from jax import lax
 from jax.sharding import PartitionSpec as P
+from jax.lax import axis_index, axis_size, ppermute
 
 HEAD_DIM = 64
 PATCHES = 196
 EPSILON = 1e-06
+
+
+def begin_works_now(field_in, shard_axis):
+    copies = []
+    base_arr, wide_out, b_next = (axis_size(shard_axis), axis_index(shard_axis), field_in.shape[2])
+    for s, hop_no in enumerate(field_in.shape):
+        copies.append(hop_no * base_arr if s == 2 else hop_no)
+    state_next = lax.dynamic_update_slice_in_dim(
+        jnp.zeros(copies, field_in.dtype), field_in, wide_out * b_next, axis=2
+    )
+    oldest = w2 = field_in
+    for dev_j in range(1, base_arr // 2 + 1):
+        line_up = []
+        for s in range(base_arr):
+            line_up.append((s, (s + 1) % base_arr))
+        oldest = ppermute(oldest, shard_axis, line_up)
+        state_next = lax.dynamic_update_slice_in_dim(
+            state_next, oldest, (wide_out - dev_j) % base_arr * b_next, axis=2
+        )
+        if 2 * dev_j < base_arr:
+            panels = []
+            for s in range(base_arr):
+                panels.append((s, (s - 1) % base_arr))
+            w2 = ppermute(w2, shard_axis, panels)
+            state_next = lax.dynamic_update_slice_in_dim(
+                state_next, w2, (wide_out + dev_j) % base_arr * b_next, axis=2
+            )
+    return state_next
+
+
+return_all_the_sources_all = functools.partial(begin_works_now, shard_axis="tensor")
 
 
 def rounded(value):
@@ -27,7 +60,7 @@
 
 
 def gather_grads(value):
-    return lax.all_gather(value, "tensor", axis=2, tiled=True)
+    return return_all_the_sources_all(value)
 
 
 def summed_grads(value):

time: 1030 us -> 1090 us (1.058)
  local copies, waits for them, and re-layouts: 204 us -> 295 us
  waiting for transfers between devices: 415 us -> 386 us
  blocking collectives: 171 us -> 145 us
  starting transfers between devices: 1.85 us -> 14.1 us
    dynamic_update_slice x0 -> x24, local copies, waits for them, and re-layouts: none -> 82.6 us  [the longest x12 39.2 us: begin_works_now(): lax.dynamic_update_slice_in_dim(state_next, oldest, (wide_out - dev_j) %...]
    all_gather x4 -> x0, blocking collectives: 38.4 us -> none  [gather_grads(): return lax.all_gather(value, 'tensor', axis=2, tiled=True)]
    unnamed x26 -> x24, waiting for transfers between devices: 233 us -> 206 us
    another operation x0 -> x14, local copies, waits for them, and re-layouts: none -> 16.1 us
    psum x2, waiting for transfers between devices: 51.6 us -> 37.9 us  [forward_tower(): lax.psum(rounded(partial_value).astype(jnp.bfloat16), 'tensor')]
    ppermute x0 -> x18, starting transfers between devices: none -> 12.7 us  [the longest x6 9.61 us: begin_works_now(): w2 = ppermute(w2, shard_axis, panels)]
    ppermute x0 -> x18, waiting for transfers between devices: none -> 12.2 us  [the longest x12 12.2 us: begin_works_now(): oldest = ppermute(oldest, shard_axis, line_up)]
    unnamed x514 -> x510, local copies, waits for them, and re-layouts: 160 us -> 155 us
  transfers between devices with their start and end apart: 16 -> 32, of which waited for: 4 -> 6; matrix products, arithmetic and copies ran while one was open for 34% -> 40% of each run, Pallas kernels for 0% -> 0%
where the time goes in v1:
time: 1090 us; the launch traced here: 1070 us
  waiting for transfers between devices  386 us (35%)
  local copies, waits for them, and re-layouts  295 us (27%)
  blocking collectives  145 us (13%)
  matrix products  114 us (10%)
  other arithmetic  97.3 us (9%)
  between operations  19.8 us (2%)
  starting transfers between devices  14.1 us (1%)
    unnamed x24, waiting for transfers between devices  206 us
    unnamed x510, local copies, waits for them, and re-layouts  155 us
    reduce_scatter x1, waiting for transfers between devices, per_device(): lax.psum_scatter(stacked[2], 'dp', scatter_dimension=1, tiled=True)  130 us
    dynamic_update_slice x12, local copies, waits for them, and re-layouts, begin_works_now(): lax.dynamic_update_slice_in_dim(state_next, oldest, (wide_out - dev_j) %...  39.2 us
    psum x1, blocking collectives, per_device(): small_grads = lax.psum(stacked[4], 'dp')  38.6 us
    psum x2, waiting for transfers between devices, forward_tower(): lax.psum(rounded(partial_value).astype(jnp.bfloat16), 'tensor')  37.9 us
    all_gather x3, blocking collectives, forward_tower(): lax.all_gather(shift, 'tensor', axis=1, tiled=True)  30.6 us
    psum x2, blocking collectives, norm_reverse_pass(): lax.psum((jnp.sum(centered_grad, axis=-1, keepdims=True), jnp.sum(centere...  26.5 us
  transfers between devices with their start and end apart: 32, of which 6 were waited for; matrix products, arithmetic and copies ran while one was open for 40% of the time, Pallas kernels for 0%

profile of v1, /device:TPU:0, one launch (start us, length us, event | category | flops | bytes accessed | tf_op | source)
XLA Modules:
  0.0 1071.7 jit_solution(18132837572147600012)
XLA Ops:
  8.2 7.9 all-gather.1
  16.1 5.3 fusion.168
  22.3 6.6 all-gather
  28.9 5.3 fusion.169
  34.4 8.7 all_gather.36
  55.5 12.6 %all_gather.40 = bf16[1,512,768]{1,2,0:T(8,128)(2,1)S(1)} all-gather(bf16[1,512,192]{1,2,0:T(8,128)(2,1)S(1)} %copy-done.79), channel_id=1, replica_groups=mesh['dp'=8,'tensor'=4] {'tensor'}, dimensions={2}, use_global_device_ids=true | all-gather | bytes 983040 | tf_op jit(solution)/shard_map/all_gather | solution.py:107
  68.6 6.6 all-gather.4
  75.2 5.3 fusion.164
  80.6 7.9 all-gather.3
  88.5 5.3 fusion.165
  108.9 16.0 %all-gather.7 = bf16[1,2,768]{1,0,2:T(2,128)(2,1)S(1)} all-gather(bf16[1,2,192]{1,0,2:T(2,128)(2,1)S(1)} %copy.288), channel_id=9, replica_groups=mesh['dp'=8,'tensor'=4] {'tensor'}, dimensions={2}, use_global_device_ids=true | all-gather | bytes 3840 | tf_op jit(solution)/shard_map/all_gather | solution.py:110
  124.9 5.4 fusion.160
  130.5 6.6 all-gather.6
  137.0 5.3 fusion.161
  146.1 7.4 all-reduce.8
  174.9 4.8 multiply_convert_fusion.5
  209.9 4.9 collective-permute-done.6
  234.8 37.9 %all-reduce.19.cloned.1.call-done = (bf16[1,512,768]{2,1,0:T(8,128)(2,1)}, bf16[1,711,768]{2,1,0:T(8,128)(2,1)}, bf16[2,197,768]{1,0,2:T(2,128)(2,1)}) async-done(((bf16[1,512,768]{2,1,0:T(8,128)(2,1)}, bf16[1,711,768]{2,1,0:T(8,128)(2,1)}, bf16[2,197,768]{1,0,2:T(2,128)(2,1)}), (bf16[1,512,768]{2,1,0:T(8,128)(2,1)}, bf16[1,711,768]{2,1,0:T(8,128)(2,1)}, ...) | async-done | bytes 2483728 | tf_op jit(solution)/shard_map/psum | solution.py:142
  275.7 6.4 multiply_convert_fusion.3
  289.1 4.8 copy.259
  298.2 7.3 collective-permute-done.12
  307.7 4.6 dynamic_update_slice.104
  315.3 4.3 dynamic_update_slice.105
  319.7 5.1 dynamic_update_slice.106
  325.9 4.4 dynamic_update_slice.107
  333.5 4.8 copy.255
  342.8 8.4 multiply_convert_fusion.2
  359.2 6.7 copy.263
  380.3 4.5 slice_reduce_fusion.4
  384.8 4.5 slice_reduce_fusion.2
  393.6 6.7 copy.257
  403.2 4.5 slice_reduce_fusion
  431.0 12.7 %all-reduce.7 = (f32[2,197]{1,0:T(2,128)}, f32[2,197,1]{1,0,2:T(2,128)}, f32[512]{0:T(512)}, f32[1,512,1]{1,2,0:T(1,128)}, f32[711]{0:T(1024)}, /*index=5*/f32[1,711,1]{1,2,0:T(1,128)}) all-reduce(f32[2,197]{1,0:T(2,128)} %get-tuple-element.87, f32[2,197,1]{1,0,2:T(2,128)} %bitcast.505, ...), channel_id=1, replica_groups=mesh['dp'=8,'tensor'=4] {'tensor'}, use_global_device_ids=true, to_apply=%region_28.29 | all-reduce | flops 3234 | bytes 25872 | tf_op jit(solution)/shard_map/psum | solution.py:73
  479.7 4.6 dynamic_update_slice.108
  497.1 4.5 dynamic_update_slice.109
  501.7 5.1 dynamic_update_slice.110
  537.8 4.7 dynamic_update_slice.111
  548.2 5.3 multiply_reduce_fusion
  562.2 5.7 copy.265
  588.4 9.8 copy.267
  598.2 11.4 %reshape.1309 = f32[768,1728]{1,0:T(8,128)} reshape(f32[768,3,3,192]{3,2,1,0:T(4,128)} %bitcast.424) | data formatting | bytes 10616832
  618.8 11.0 %copy.271 = f32[3,768,768]{1,0,2:T(4,128)} copy(f32[3,768,768]{2,1,0:T(8,128)} %pad_maximum_fusion.1) | data formatting | bytes 14155776
  629.9 8.2 copy.289
  659.1 13.8 %all-reduce.6 = (f32[2,197]{1,0:T(2,128)S(1)}, f32[2,197,1]{1,0,2:T(2,128)S(1)}, f32[512]{0:T(512)S(1)}, f32[1,512,1]{1,2,0:T(1,128)S(1)}, f32[711]{0:T(1024)S(1)}, /*index=5*/f32[1,711,1]{1,2,0:T(1,128)S(1)}) all-reduce(f32[2,197]{1,0:T(2,128)S(1)} %get-tuple-element.105, ...), channel_id=1, replica_groups=mesh['dp'=8,'tensor'=4] {'tensor'}, use_global_device_ids=true, to_apply=%region_34.35 | all-reduce | flops 3234 | bytes 25872 | tf_op jit(solution)/shard_map/psum | solution.py:73
  680.9 38.6 %psum.127 = f32[3,12,192]{2,1,0:T(8,128)S(1)} all-reduce(f32[3,12,192]{2,1,0:T(8,128)S(1)} %pad_maximum_fusion.9), channel_id=1, replica_groups=mesh['dp'=8,'tensor'=4] {'dp'}, use_global_device_ids=true, to_apply=%region_85.86 | all-reduce | flops 6912 | bytes 55296 | tf_op jit(solution)/shard_map/psum | solution.py:360
  723.4 76.6 %reduce-scatter.43.cloned.1.call-done = f32[96,1728]{1,0:T(8,128)} async-done(((f32[768,1728]{1,0:T(8,128)}), f32[96,1728]{1,0:T(8,128)}) %reduce-scatter.43.cloned.1.call-update) | async-done | bytes 663568
  802.9 129.4 %reduce-scatter.47.cloned.1.call-done = f32[96,2304]{1,0:T(8,128)} async-done(((f32[768,2304]{1,0:T(8,128)}), f32[96,2304]{1,0:T(8,128)}) %reduce-scatter.47.cloned.1.call-update) | async-done | bytes 884752
  935.0 129.8 %reduce-scatter.29.cloned.1.call-done = f32[3,96,768]{2,1,0:T(8,128)} async-done(((f32[3,768,768]{2,1,0:T(8,128)}), f32[3,96,768]{2,1,0:T(8,128)}) %reduce-scatter.29.cloned.1.call-update) | async-done | bytes 884752 | tf_op jit(solution)/shard_map/reduce_scatter | solution.py:357
  (760 shorter events, 343.7 us)
Async XLA Ops:
  7.2 27.0 %copy-start.73 = (bf16[2,197,192]{1,2,0:T(8,128)(2,1)S(1)}, bf16[2,197,192]{1,2,0:T(8,128)(2,1)}, u32[]{:S(2)}) copy-start(bf16[2,197,192]{1,2,0:T(8,128)(2,1)} %param.18) | copy-start | bytes 453892
  7.2 158.3 %all-reduce.15.cloned.1.call-start = ((), (), s32[]{:S(2)}) async-start(), calls=%async_computation.10 | async-start | bytes 1228800 | tf_op jit(solution)/shard_map/psum | solution.py:142
  21.4 22.6 %copy-start.164 = (f32[768]{0:T(1024)}, f32[768]{0:T(1024)S(1)}, u32[]{:S(2)}) copy-start(f32[768]{0:T(1024)S(1)} %get-tuple-element.116) | copy-start | bytes 9220
  51.1 138.1 %all-gather.11.cloned.1.call-start = ((), (), s32[]{:S(2)}) async-start(), calls=%async_computation.11 | async-start | bytes 1474560 | tf_op jit(solution)/shard_map/all_gather | solution.py:107
  51.1 107.7 %collective-permute-start = (bf16[2,197,192]{1,2,0:T(8,128)(2,1)}, bf16[2,197,192]{1,2,0:T(8,128)(2,1)}, u32[]{:S(2)}, u32[]{:S(2)}) collective-permute-start(bf16[2,197,192]{1,2,0:T(8,128)(2,1)} %param.33), channel_id=1, source_target_pairs={{0,1},{1,2},{2,3},{3,0},{4,5},{5,6},{6,7},{7,4},{8,9},{9,10},{10,1... | collective-permute-start | bytes 453896 | tf_op jit(solution)/shard_map/ppermute | solution.py:27
  51.5 110.4 %collective-permute-start.1 = (bf16[2,197,192]{1,2,0:T(8,128)(2,1)}, bf16[2,197,192]{1,2,0:T(8,128)(2,1)}, u32[]{:S(2)}, u32[]{:S(2)}) collective-permute-start(bf16[2,197,192]{1,2,0:T(8,128)(2,1)} %param.33), channel_id=1, source_target_pairs={{0,3},{1,0},{2,1},{3,2},{4,7},{5,4},{6,5},{7,6},{8,11},{9,8},{10,9... | collective-permute-start | bytes 453896 | tf_op jit(solution)/shard_map/ppermute | solution.py:35
  53.0 219.8 %all-reduce.19.cloned.1.call-start = ((), (), s32[]{:S(2)}) async-start(), calls=%async_computation.23 | async-start | bytes 5332992 | tf_op jit(solution)/shard_map/psum | solution.py:142
  68.4 25.8 %copy-start.7 = (bf16[1,512,768]{2,1,0:T(8,128)(2,1)}, bf16[1,512,768]{2,1,0:T(8,128)(2,1)S(1)}, u32[]{:S(2)}) copy-start(bf16[1,512,768]{2,1,0:T(8,128)(2,1)S(1)} %copy.191) | copy-start | bytes 2359300
  108.8 35.3 %copy-start.209 = (u32[32]{0:T(128)S(1)}, u32[32]{0:T(128)}, u32[]{:S(2)}) copy-start(u32[32]{0:T(128)} %constant.272) | copy-start | bytes 388
  108.8 36.6 %copy-start.212 = (bf16[192]{0:T(256)(128)(2,1)S(1)}, bf16[192]{0:T(256)(128)(2,1)}, u32[]{:S(2)}) copy-start(bf16[192]{0:T(256)(128)(2,1)} %get-tuple-element.146) | copy-start | bytes 1156
  108.8 36.8 %copy-start.211 = (bf16[192]{0:T(256)(128)(2,1)S(1)}, bf16[192]{0:T(256)(128)(2,1)}, u32[]{:S(2)}) copy-start(bf16[192]{0:T(256)(128)(2,1)} %get-tuple-element.147) | copy-start | bytes 1156
  108.8 37.0 %copy-start.210 = (bf16[192]{0:T(256)(128)(2,1)S(1)}, bf16[192]{0:T(256)(128)(2,1)}, u32[]{:S(2)}) copy-start(bf16[192]{0:T(256)(128)(2,1)} %get-tuple-element.145) | copy-start | bytes 1156
  108.8 45.2 %copy-start.199 = (f32[192]{0:T(256)S(1)}, f32[192]{0:T(256)}, u32[]{:S(2)}) copy-start(f32[192]{0:T(256)} %get-tuple-element.144) | copy-start | bytes 2308
  108.9 45.9 %copy-start.198 = (f32[192]{0:T(256)S(1)}, f32[192]{0:T(256)}, u32[]{:S(2)}) copy-start(f32[192]{0:T(256)} %get-tuple-element.139) | copy-start | bytes 2308
  130.3 27.9 %copy-start.142 = (bf16[3,768]{1,0:T(4,128)(2,1)S(1)}, bf16[3,768]{1,0:T(4,128)(2,1)}, u32[]{:S(2)}) copy-start(bf16[3,768]{1,0:T(4,128)(2,1)} %param.28) | copy-start | bytes 13828
  144.0 24.3 %copy-start.32 = (bf16[2,197,192]{2,1,0:T(8,128)(2,1)}, bf16[2,197,192]{2,1,0:T(8,128)(2,1)S(1)}, u32[]{:S(2)}) copy-start(bf16[2,197,192]{2,1,0:T(8,128)(2,1)S(1)} %copy.200) | copy-start | bytes 453892
  165.5 7.2 collective-permute-start.2
  207.4 206.3 %reduce-scatter.35.cloned.1.call-start = ((), (), s32[]{:S(2)}) async-start(), calls=%async_computation.15 | async-start | bytes 983040
  207.4 7.4 collective-permute-start.6
  208.6 13.1 %collective-permute-start.7 = (bf16[1,512,192]{1,2,0:T(8,128)(2,1)}, bf16[1,512,192]{1,2,0:T(8,128)(2,1)}, u32[]{:S(2)}, u32[]{:S(2)}) collective-permute-start(bf16[1,512,192]{1,2,0:T(8,128)(2,1)} %param.34), channel_id=1, source_target_pairs={{0,3},{1,0},{2,1},{3,2},{4,7},{5,4},{6,5},{7,6},{8,11},{9,8},{10,9... | collective-permute-start | bytes 589832 | tf_op jit(solution)/shard_map/ppermute | solution.py:35
  214.8 15.7 %collective-permute-start.8 = (bf16[1,512,192]{1,2,0:T(8,128)(2,1)}, bf16[1,512,192]{1,2,0:T(8,128)(2,1)}, u32[]{:S(2)}, u32[]{:S(2)}) collective-permute-start(bf16[1,512,192]{1,2,0:T(8,128)(2,1)} %collective-permute-done.6), channel_id=1, source_target_pairs={{0,1},{1,2},{2,3},{3,0},{4,5},{5,6},{6,7},{7,4},{8,9},{9,10},{10,1... | collective-permute-start | bytes 589832 | tf_op jit(solution)/shard_map/ppermute | solution.py:27
  214.8 60.9 %copy-start.138 = (f32[768]{0:T(1024)}, f32[768]{0:T(1024)S(1)}, u32[]{:S(2)}) copy-start(f32[768]{0:T(1024)S(1)} %convert_element_type.888) | copy-start | bytes 9220
  296.4 121.0 %reduce-scatter.31.cloned.1.call-start = ((), (), s32[]{:S(2)}) async-start(), calls=%async_computation.13 | async-start | bytes 983040
  296.4 9.1 collective-permute-start.12
  296.5 17.0 %collective-permute-start.13 = (bf16[1,711,192]{1,2,0:T(8,128)(2,1)}, bf16[1,711,192]{1,2,0:T(8,128)(2,1)}, u32[]{:S(2)}, u32[]{:S(2)}) collective-permute-start(bf16[1,711,192]{1,2,0:T(8,128)(2,1)} %param.35), channel_id=1, source_target_pairs={{0,3},{1,0},{2,1},{3,2},{4,7},{5,4},{6,5},{7,6},{8,11},{9,8},{10,9... | collective-permute-start | bytes 819080 | tf_op jit(solution)/shard_map/ppermute | solution.py:35
  305.5 19.3 %collective-permute-start.14 = (bf16[1,711,192]{1,2,0:T(8,128)(2,1)}, bf16[1,711,192]{1,2,0:T(8,128)(2,1)}, u32[]{:S(2)}, u32[]{:S(2)}) collective-permute-start(bf16[1,711,192]{1,2,0:T(8,128)(2,1)} %collective-permute-done.12), channel_id=1, source_target_pairs={{0,1},{1,2},{2,3},{3,0},{4,5},{5,6},{6,7},{7,4},{8,9},{9,10},{10,1... | collective-permute-start | bytes 819080 | tf_op jit(solution)/shard_map/ppermute | solution.py:27
  305.5 37.3 %copy-start.140 = (f32[768]{0:T(1024)}, f32[768]{0:T(1024)S(1)}, u32[]{:S(2)}) copy-start(f32[768]{0:T(1024)S(1)} %convert_element_type.889) | copy-start | bytes 9220
  342.7 80.9 %reduce-scatter.39.cloned.1.call-start = ((), (), s32[]{:S(2)}) async-start(), calls=%async_computation.17 | async-start | bytes 1474560
  368.9 86.7 %reduce-scatter.33.cloned.1.call-start = ((), (), s32[]{:S(2)}) async-start(), calls=%async_computation.14 | async-start | bytes 1474560
  369.9 19.4 %copy-start.159 = (bf16[3,192]{1,0:T(4,128)(2,1)S(1)}, bf16[3,192]{1,0:T(4,128)(2,1)}, u32[]{:S(2)}) copy-start(bf16[3,192]{1,0:T(4,128)(2,1)} %param.30) | copy-start | bytes 3460
  384.8 26.4 %copy-start.134 = (f32[192]{0:T(256)}, f32[192]{0:T(256)S(1)}, u32[]{:S(2)}) copy-start(f32[192]{0:T(256)S(1)} %get-tuple-element.135) | copy-start | bytes 2308
  403.1 248.0 %all-reduce.17.cloned.1.call-start = ((), (), s32[]{:S(2)}) async-start(), calls=%async_computation.22 | async-start | bytes 3145728
  447.3 16.4 %collective-permute-start.3 = (bf16[2,197,192]{2,1,0:T(8,128)(2,1)}, bf16[2,197,192]{2,1,0:T(8,128)(2,1)}, u32[]{:S(2)}, u32[]{:S(2)}) collective-permute-start(bf16[2,197,192]{2,1,0:T(8,128)(2,1)} %get-tuple-element.169), channel_id=1, source_target_pairs={{0,1},{1,2},{2,3},{3,0},{4,5},{5,6},{6,7},{7,4},{8,9},{9,10},{10,1... | collective-permute-start | bytes 453896 | tf_op jit(solution)/shard_map/ppermute | solution.py:27
  447.3 18.2 %collective-permute-start.4 = (bf16[2,197,192]{2,1,0:T(8,128)(2,1)}, bf16[2,197,192]{2,1,0:T(8,128)(2,1)}, u32[]{:S(2)}, u32[]{:S(2)}) collective-permute-start(bf16[2,197,192]{2,1,0:T(8,128)(2,1)} %get-tuple-element.169), channel_id=1, source_target_pairs={{0,3},{1,0},{2,1},{3,2},{4,7},{5,4},{6,5},{7,6},{8,11},{9,8},{10,9... | collective-permute-start | bytes 453896 | tf_op jit(solution)/shard_map/ppermute | solution.py:35
  453.3 35.8 %collective-permute-start.9 = (bf16[1,512,192]{2,1,0:T(8,128)(2,1)}, bf16[1,512,192]{2,1,0:T(8,128)(2,1)}, u32[]{:S(2)}, u32[]{:S(2)}) collective-permute-start(bf16[1,512,192]{2,1,0:T(8,128)(2,1)} %get-tuple-element.171), channel_id=1, source_target_pairs={{0,1},{1,2},{2,3},{3,0},{4,5},{5,6},{6,7},{7,4},{8,9},{9,10},{10,1... | collective-permute-start | bytes 589832 | tf_op jit(solution)/shard_map/ppermute | solution.py:27
  453.8 38.5 %collective-permute-start.10 = (bf16[1,512,192]{2,1,0:T(8,128)(2,1)}, bf16[1,512,192]{2,1,0:T(8,128)(2,1)}, u32[]{:S(2)}, u32[]{:S(2)}) collective-permute-start(bf16[1,512,192]{2,1,0:T(8,128)(2,1)} %get-tuple-element.171), channel_id=1, source_target_pairs={{0,3},{1,0},{2,1},{3,2},{4,7},{5,4},{6,5},{7,6},{8,11},{9,8},{10,9... | collective-permute-start | bytes 589832 | tf_op jit(solution)/shard_map/ppermute | solution.py:35
  463.7 33.4 %collective-permute-start.15 = (bf16[1,711,192]{2,1,0:T(8,128)(2,1)}, bf16[1,711,192]{2,1,0:T(8,128)(2,1)}, u32[]{:S(2)}, u32[]{:S(2)}) collective-permute-start(bf16[1,711,192]{2,1,0:T(8,128)(2,1)} %get-tuple-element.174), channel_id=1, source_target_pairs={{0,1},{1,2},{2,3},{3,0},{4,5},{5,6},{6,7},{7,4},{8,9},{9,10},{10,1... | collective-permute-start | bytes 819080 | tf_op jit(solution)/shard_map/ppermute | solution.py:27
  463.8 37.9 %collective-permute-start.16 = (bf16[1,711,192]{2,1,0:T(8,128)(2,1)}, bf16[1,711,192]{2,1,0:T(8,128)(2,1)}, u32[]{:S(2)}, u32[]{:S(2)}) collective-permute-start(bf16[1,711,192]{2,1,0:T(8,128)(2,1)} %get-tuple-element.174), channel_id=1, source_target_pairs={{0,3},{1,0},{2,1},{3,2},{4,7},{5,4},{6,5},{7,6},{8,11},{9,8},{10,9... | collective-permute-start | bytes 819080 | tf_op jit(solution)/shard_map/ppermute | solution.py:35
  465.5 41.3 %collective-permute-start.5 = (bf16[2,197,192]{2,1,0:T(8,128)(2,1)}, bf16[2,197,192]{2,1,0:T(8,128)(2,1)}, u32[]{:S(2)}, u32[]{:S(2)}) collective-permute-start(bf16[2,197,192]{2,1,0:T(8,128)(2,1)} %collective-permute-done.3), channel_id=1, source_target_pairs={{0,1},{1,2},{2,3},{3,0},{4,5},{5,6},{6,7},{7,4},{8,9},{9,10},{10,1... | collective-permute-start | bytes 453896 | tf_op jit(solution)/shard_map/ppermute | solution.py:27
  496.2 24.6 %collective-permute-start.11 = (bf16[1,512,192]{2,1,0:T(8,128)(2,1)}, bf16[1,512,192]{2,1,0:T(8,128)(2,1)}, u32[]{:S(2)}, u32[]{:S(2)}) collective-permute-start(bf16[1,512,192]{2,1,0:T(8,128)(2,1)} %collective-permute-done.9), channel_id=1, source_target_pairs={{0,1},{1,2},{2,3},{3,0},{4,5},{5,6},{6,7},{7,4},{8,9},{9,10},{10,1... | collective-permute-start | bytes 589832 | tf_op jit(solution)/shard_map/ppermute | solution.py:27
  506.8 30.6 %collective-permute-start.17 = (bf16[1,711,192]{2,1,0:T(8,128)(2,1)}, bf16[1,711,192]{2,1,0:T(8,128)(2,1)}, u32[]{:S(2)}, u32[]{:S(2)}) collective-permute-start(bf16[1,711,192]{2,1,0:T(8,128)(2,1)} %collective-permute-done.15), channel_id=1, source_target_pairs={{0,1},{1,2},{2,3},{3,0},{4,5},{5,6},{6,7},{7,4},{8,9},{9,10},{10,1... | collective-permute-start | bytes 819080 | tf_op jit(solution)/shard_map/ppermute | solution.py:27
  520.6 133.6 %reduce-scatter.37.cloned.1.call-start = ((), (), s32[]{:S(2)}) async-start(), calls=%async_computation.16 | async-start | bytes 983040
  537.4 119.0 %reduce-scatter.41.cloned.1.call-start = ((), (), s32[]{:S(2)}) async-start(), calls=%async_computation.18 | async-start | bytes 1474560
  569.3 152.2 %reduce-scatter.45.cloned.1.call-start = ((), (), s32[]{:S(2)}) async-start(), calls=%async_computation.20 | async-start | bytes 2211840
  580.0 220.1 %reduce-scatter.43.cloned.1.call-start = ((), (), s32[]{:S(2)}) async-start(), calls=%async_computation.19 | async-start | bytes 6193152
  609.7 322.6 %reduce-scatter.47.cloned.1.call-start = ((), (), s32[]{:S(2)}) async-start(), calls=%async_computation.21 | async-start | bytes 7962624
  638.1 426.6 %reduce-scatter.29.cloned.1.call-start = ((), (), s32[]{:S(2)}) async-start(), calls=%async_computation.12 | async-start | bytes 7962624 | tf_op jit(solution)/shard_map/reduce_scatter | solution.py:357
  658.5 19.7 %copy-start.43 = (f32[1,512,192]{2,1,0:T(8,128)S(1)}, f32[1,512,192]{2,1,0:T(8,128)}, u32[]{:S(2)}) copy-start(f32[1,512,192]{2,1,0:T(8,128)} %get-tuple-element.172) | copy-start | bytes 1179652
  (206 other events, 764.6 us)
Sparse Core Ops, SparseCore 0:
  51.2 37.0 all-reduce.14
  89.9 18.1 all-gather.10
  207.5 65.1 all-reduce.18
  296.5 23.2 reduce-scatter.34
  342.8 24.2 reduce-scatter.30
  369.6 26.0 reduce-scatter.38
  403.3 26.6 reduce-scatter.32
  520.7 44.5 all-reduce.16
  567.8 23.2 reduce-scatter.36
  593.5 25.6 reduce-scatter.40
  622.7 67.8 reduce-scatter.44
  694.0 105.9 reduce-scatter.42
  803.7 128.5 reduce-scatter.46
  936.4 128.2 reduce-scatter.28
